TPU v7x, 32 devices: a whole 2x2x4 slice. The times are simulated.
32 devices in a mesh: rep: 4 (over x, core), row: 2 (over y), col: 4 (over z).
Axes of the slice: x: 2, y: 2, z: 4, core: 2. Of those that a mesh axis runs over, the one named last changes fastest.
Arguments:
- spin_init: bfloat16 [256, 8192], P('rep', 'row'), may hold values from -1 to 1, as said below
- couplings: bfloat16 [2, 4, 1024, 8192], P(None, 'col', None, 'row'), may hold values from -1 to 1, as said below
- flip_noise: float32 [10, 256, 8192], P(None, 'rep', 'row'), may hold values from 0 to 17, as said below
- colors: int32 [8192], P('row'), may hold values 0 or 1
- beta_steps: int32 [256], replicated, may hold values from 96 to 1024
- partners: int32 [256], replicated, may hold values from 0 to 255, as said below
- swap_noise: float32 [256], replicated, may hold values from 0 to 17, as said below
Outputs:
- spins_out: bfloat16 [256, 8192], P('rep', 'row')
- energies: float32 [256], P('rep')
Inputs may be any that keep to these rules, and one draw needn't show every extreme that they name: `spin_init`: every entry is -1 or +1. `couplings`: the 8192 x 8192 matrix is symmetric, zero on its diagonal, and every other entry is -1 or +1. `flip_noise`: independent exponential variates of mean one. `swap_noise`: independent exponential variates of mean one. Pairs slots: partners[partners[r]] = r and partners[r] != r for every slot.
All inputs are finite; a program needn't handle non-finite values. No bound on the sum of `colors` on one device may be relied on, other than what follows from the above.
Results may differ from a plain program's by a relative error of at most 0.001.
Values may be sent and summed in bfloat16 or wider, within the bound.
A program may use at most 64 MiB of HBM per device.

v0:
```python
import math

import jax
import jax.numpy as jnp
from jax import lax
from jax.sharding import PartitionSpec as P

N = 8192
SWEEPS = 10


def metropolis(spin_state, fields, parity, color_part, noise_part, beta_col):
    values = spin_state.astype(jnp.float32)
    energy_cost = beta_col * (values * fields) * (1.0 / 16384.0)
    flipped = (color_part == parity)[None, :] & (energy_cost < noise_part)
    return jnp.where(flipped, -values, values).astype(jnp.bfloat16)


def partial_fields(strided, coupling_block):
    return jnp.dot(strided, coupling_block, preferred_element_type=jnp.float32)


def per_device(spin_init, couplings, flip_noise, colors, beta_steps, partners, swap_noise):
    rep_dev, row_width = spin_init.shape
    col_count = lax.axis_size("col")
    col_index = lax.axis_index("col")
    rep_index = lax.axis_index("rep")
    piece_size = row_width // col_count
    coupling_block = couplings.reshape(-1, row_width)
    beta_col = lax.dynamic_slice_in_dim(beta_steps, rep_index * rep_dev, rep_dev).astype(
        jnp.float32
    )[:, None]
    color_part = lax.dynamic_slice_in_dim(colors, col_index * piece_size, piece_size)
    noise_part = lax.dynamic_slice_in_dim(flip_noise, col_index * piece_size, piece_size, 2)

    def strided_of(spin_state):
        return lax.all_gather(spin_state, "row", axis=1, tiled=True)

    def one_sweep(step_index, spin_state):
        terms = partial_fields(strided_of(spin_state), coupling_block)
        fields = lax.psum_scatter(terms, "col", scatter_dimension=1, tiled=True)
        return metropolis(
            spin_state, fields, step_index % 2, color_part, noise_part[step_index], beta_col
        )

    start_pieces = lax.dynamic_slice_in_dim(spin_init, col_index * piece_size, piece_size, 1)
    final_pieces = lax.fori_loop(0, SWEEPS, one_sweep, start_pieces)
    strided = strided_of(final_pieces)
    final_rows = lax.all_gather(final_pieces, "col", axis=1, tiled=True)
    every_spins = lax.all_gather(final_rows, "rep", axis=0, tiled=True)
    final_partial = partial_fields(strided, coupling_block)
    row_values = final_rows.astype(jnp.float32)
    final_local = lax.psum(final_partial, "col")
    total_sum = lax.psum(jnp.sum(row_values * final_local, axis=1), "row")
    energy = -0.5 * total_sum
    every_energy = lax.all_gather(energy, "rep", axis=0, tiled=True)
    slot_ids = rep_index * rep_dev + jnp.arange(rep_dev, dtype=jnp.int32)
    mate_ids = lax.dynamic_slice_in_dim(partners, rep_index * rep_dev, rep_dev)
    all_betas = beta_steps.astype(jnp.float32)
    mate_energy = every_energy[mate_ids]
    swap_gain = (
        (beta_col[:, 0] - all_betas[mate_ids])
        * (energy - mate_energy)
        * (1.0 / (64.0 * N * math.sqrt(N)))
    )
    accept = swap_gain + swap_noise[jnp.minimum(slot_ids, mate_ids)] > 0.0
    spins_out = jnp.where(accept[:, None], every_spins[mate_ids], final_rows)
    energies = jnp.where(accept, mate_energy, energy) * (1.0 / (N * math.sqrt(N)))
    return (spins_out, energies)


def solution(mesh):
    in_specs = (
        P("rep", "row"),
        P(None, "col", None, "row"),
        P(None, "rep", "row"),
        P("row"),
        P(),
        P(),
        P(),
    )
    out_specs = (P("rep", "row"), P("rep"))
    return jax.shard_map(
        per_device, mesh=mesh, in_specs=in_specs, out_specs=out_specs, check_vma=False
    )
```

profile of v0, /device:TPU:0, one launch (start us, length us, event | category | flops | bytes accessed | tf_op | source)
XLA Modules:
  0.0 540.9 jit_solution(17251068194962414624)
XLA Ops:
  9.8 1.9 constant_dynamic-slice_fusion
  12.4 431.6 %while.15 = (s32[]{:T(128)}, bf16[64,1024]{1,0:T(8,128)(2,1)S(1)}, s32[1024]{0:T(1024)S(1)}, f32[64,1]{0,1:T(1,128)S(1)}, bf16[2048,4096]{1,0:T(8,128)(2,1)}, /*...) while((s32[]{:T(128)}, bf16[64,1024]{1,0:T(8,128)(2,1)S(1)}, s32[1024]{0:T(1024)S(1)}, ...), condition=%wide.region_2.3_spmd, body=%wide.region_0.2_spmd.sunk | while | flops 1074332672 | bytes 23206348 | solution.py:47
  12.4 7.1 %all_gather.27 = bf16[64,2048]{1,0:T(8,128)(2,1)S(1)} all-gather(bf16[64,1024]{1,0:T(8,128)(2,1)S(1)} %get-tuple-element.221), channel_id=1, replica_groups=mesh['rep'=4,'row'=2,'col'=4] {'row'}, dimensions={1}, use_global_device_ids=true | all-gather | bytes 393216 | tf_op jit(solution)/shard_map/while/body/eval_jaxpr/all_gather | solution.py:37
  19.6 9.8 %fusion.17 = f32[64,4096]{1,0:T(8,128)} fusion(bf16[64,2048]{1,0:T(8,128)(2,1)S(1)} %all_gather.27, bf16[2048,4096]{1,0:T(8,128)(2,1)} %get-tuple-element.233), kind=kOutput, calls=%fused_computation.24.clone.1 | convolution fusion | flops 1073741824 | bytes 18087936 | tf_op jit(solution)/shard_map/while/body/eval_jaxpr/dot_general | solution.py:20
  29.4 28.9 %reduce-scatter.2.cloned.1.call-done = f32[64,1024]{1,0:T(8,128)} async-done(((f32[64,4096]{1,0:T(8,128)}), f32[64,1024]{1,0:T(8,128)}) %reduce-scatter.2.cloned.1.call-update) | async-done | bytes 262160 | tf_op jit(solution)/shard_map/while/body/eval_jaxpr/reduce_scatter | solution.py:41
  58.3 1.1 fusion.18
  59.4 5.6 %all_gather.27 = bf16[64,2048]{1,0:T(8,128)(2,1)S(1)} all-gather(bf16[64,1024]{1,0:T(8,128)(2,1)S(1)} %get-tuple-element.221), channel_id=1, replica_groups=mesh['rep'=4,'row'=2,'col'=4] {'row'}, dimensions={1}, use_global_device_ids=true | all-gather | bytes 393216 | tf_op jit(solution)/shard_map/while/body/eval_jaxpr/all_gather | solution.py:37
  65.1 9.8 %fusion.17 = f32[64,4096]{1,0:T(8,128)} fusion(bf16[64,2048]{1,0:T(8,128)(2,1)S(1)} %all_gather.27, bf16[2048,4096]{1,0:T(8,128)(2,1)} %get-tuple-element.233), kind=kOutput, calls=%fused_computation.24.clone.1 | convolution fusion | flops 1073741824 | bytes 18087936 | tf_op jit(solution)/shard_map/while/body/eval_jaxpr/dot_general | solution.py:20
  74.9 26.1 %reduce-scatter.2.cloned.1.call-done = f32[64,1024]{1,0:T(8,128)} async-done(((f32[64,4096]{1,0:T(8,128)}), f32[64,1024]{1,0:T(8,128)}) %reduce-scatter.2.cloned.1.call-update) | async-done | bytes 262160 | tf_op jit(solution)/shard_map/while/body/eval_jaxpr/reduce_scatter | solution.py:41
  101.0 1.1 fusion.18
  102.2 5.6 %all_gather.27 = bf16[64,2048]{1,0:T(8,128)(2,1)S(1)} all-gather(bf16[64,1024]{1,0:T(8,128)(2,1)S(1)} %get-tuple-element.221), channel_id=1, replica_groups=mesh['rep'=4,'row'=2,'col'=4] {'row'}, dimensions={1}, use_global_device_ids=true | all-gather | bytes 393216 | tf_op jit(solution)/shard_map/while/body/eval_jaxpr/all_gather | solution.py:37
  107.8 9.8 %fusion.17 = f32[64,4096]{1,0:T(8,128)} fusion(bf16[64,2048]{1,0:T(8,128)(2,1)S(1)} %all_gather.27, bf16[2048,4096]{1,0:T(8,128)(2,1)} %get-tuple-element.233), kind=kOutput, calls=%fused_computation.24.clone.1 | convolution fusion | flops 1073741824 | bytes 18087936 | tf_op jit(solution)/shard_map/while/body/eval_jaxpr/dot_general | solution.py:20
  117.6 26.1 %reduce-scatter.2.cloned.1.call-done = f32[64,1024]{1,0:T(8,128)} async-done(((f32[64,4096]{1,0:T(8,128)}), f32[64,1024]{1,0:T(8,128)}) %reduce-scatter.2.cloned.1.call-update) | async-done | bytes 262160 | tf_op jit(solution)/shard_map/while/body/eval_jaxpr/reduce_scatter | solution.py:41
  143.8 1.1 fusion.18
  144.9 5.6 %all_gather.27 = bf16[64,2048]{1,0:T(8,128)(2,1)S(1)} all-gather(bf16[64,1024]{1,0:T(8,128)(2,1)S(1)} %get-tuple-element.221), channel_id=1, replica_groups=mesh['rep'=4,'row'=2,'col'=4] {'row'}, dimensions={1}, use_global_device_ids=true | all-gather | bytes 393216 | tf_op jit(solution)/shard_map/while/body/eval_jaxpr/all_gather | solution.py:37
  150.5 9.8 %fusion.17 = f32[64,4096]{1,0:T(8,128)} fusion(bf16[64,2048]{1,0:T(8,128)(2,1)S(1)} %all_gather.27, bf16[2048,4096]{1,0:T(8,128)(2,1)} %get-tuple-element.233), kind=kOutput, calls=%fused_computation.24.clone.1 | convolution fusion | flops 1073741824 | bytes 18087936 | tf_op jit(solution)/shard_map/while/body/eval_jaxpr/dot_general | solution.py:20
  160.4 26.2 %reduce-scatter.2.cloned.1.call-done = f32[64,1024]{1,0:T(8,128)} async-done(((f32[64,4096]{1,0:T(8,128)}), f32[64,1024]{1,0:T(8,128)}) %reduce-scatter.2.cloned.1.call-update) | async-done | bytes 262160 | tf_op jit(solution)/shard_map/while/body/eval_jaxpr/reduce_scatter | solution.py:41
  186.5 1.1 fusion.18
  187.7 5.6 %all_gather.27 = bf16[64,2048]{1,0:T(8,128)(2,1)S(1)} all-gather(bf16[64,1024]{1,0:T(8,128)(2,1)S(1)} %get-tuple-element.221), channel_id=1, replica_groups=mesh['rep'=4,'row'=2,'col'=4] {'row'}, dimensions={1}, use_global_device_ids=true | all-gather | bytes 393216 | tf_op jit(solution)/shard_map/while/body/eval_jaxpr/all_gather | solution.py:37
  193.3 9.8 %fusion.17 = f32[64,4096]{1,0:T(8,128)} fusion(bf16[64,2048]{1,0:T(8,128)(2,1)S(1)} %all_gather.27, bf16[2048,4096]{1,0:T(8,128)(2,1)} %get-tuple-element.233), kind=kOutput, calls=%fused_computation.24.clone.1 | convolution fusion | flops 1073741824 | bytes 18087936 | tf_op jit(solution)/shard_map/while/body/eval_jaxpr/dot_general | solution.py:20
  203.1 26.1 %reduce-scatter.2.cloned.1.call-done = f32[64,1024]{1,0:T(8,128)} async-done(((f32[64,4096]{1,0:T(8,128)}), f32[64,1024]{1,0:T(8,128)}) %reduce-scatter.2.cloned.1.call-update) | async-done | bytes 262160 | tf_op jit(solution)/shard_map/while/body/eval_jaxpr/reduce_scatter | solution.py:41
  230.4 5.6 %all_gather.27 = bf16[64,2048]{1,0:T(8,128)(2,1)S(1)} all-gather(bf16[64,1024]{1,0:T(8,128)(2,1)S(1)} %get-tuple-element.221), channel_id=1, replica_groups=mesh['rep'=4,'row'=2,'col'=4] {'row'}, dimensions={1}, use_global_device_ids=true | all-gather | bytes 393216 | tf_op jit(solution)/shard_map/while/body/eval_jaxpr/all_gather | solution.py:37
  236.0 9.8 %fusion.17 = f32[64,4096]{1,0:T(8,128)} fusion(bf16[64,2048]{1,0:T(8,128)(2,1)S(1)} %all_gather.27, bf16[2048,4096]{1,0:T(8,128)(2,1)} %get-tuple-element.233), kind=kOutput, calls=%fused_computation.24.clone.1 | convolution fusion | flops 1073741824 | bytes 18087936 | tf_op jit(solution)/shard_map/while/body/eval_jaxpr/dot_general | solution.py:20
  245.8 26.1 %reduce-scatter.2.cloned.1.call-done = f32[64,1024]{1,0:T(8,128)} async-done(((f32[64,4096]{1,0:T(8,128)}), f32[64,1024]{1,0:T(8,128)}) %reduce-scatter.2.cloned.1.call-update) | async-done | bytes 262160 | tf_op jit(solution)/shard_map/while/body/eval_jaxpr/reduce_scatter | solution.py:41
  273.1 5.6 %all_gather.27 = bf16[64,2048]{1,0:T(8,128)(2,1)S(1)} all-gather(bf16[64,1024]{1,0:T(8,128)(2,1)S(1)} %get-tuple-element.221), channel_id=1, replica_groups=mesh['rep'=4,'row'=2,'col'=4] {'row'}, dimensions={1}, use_global_device_ids=true | all-gather | bytes 393216 | tf_op jit(solution)/shard_map/while/body/eval_jaxpr/all_gather | solution.py:37
  278.8 9.8 %fusion.17 = f32[64,4096]{1,0:T(8,128)} fusion(bf16[64,2048]{1,0:T(8,128)(2,1)S(1)} %all_gather.27, bf16[2048,4096]{1,0:T(8,128)(2,1)} %get-tuple-element.233), kind=kOutput, calls=%fused_computation.24.clone.1 | convolution fusion | flops 1073741824 | bytes 18087936 | tf_op jit(solution)/shard_map/while/body/eval_jaxpr/dot_general | solution.py:20
  288.6 26.1 %reduce-scatter.2.cloned.1.call-done = f32[64,1024]{1,0:T(8,128)} async-done(((f32[64,4096]{1,0:T(8,128)}), f32[64,1024]{1,0:T(8,128)}) %reduce-scatter.2.cloned.1.call-update) | async-done | bytes 262160 | tf_op jit(solution)/shard_map/while/body/eval_jaxpr/reduce_scatter | solution.py:41
  314.7 1.1 fusion.18
  315.9 5.6 %all_gather.27 = bf16[64,2048]{1,0:T(8,128)(2,1)S(1)} all-gather(bf16[64,1024]{1,0:T(8,128)(2,1)S(1)} %get-tuple-element.221), channel_id=1, replica_groups=mesh['rep'=4,'row'=2,'col'=4] {'row'}, dimensions={1}, use_global_device_ids=true | all-gather | bytes 393216 | tf_op jit(solution)/shard_map/while/body/eval_jaxpr/all_gather | solution.py:37
  321.5 9.8 %fusion.17 = f32[64,4096]{1,0:T(8,128)} fusion(bf16[64,2048]{1,0:T(8,128)(2,1)S(1)} %all_gather.27, bf16[2048,4096]{1,0:T(8,128)(2,1)} %get-tuple-element.233), kind=kOutput, calls=%fused_computation.24.clone.1 | convolution fusion | flops 1073741824 | bytes 18087936 | tf_op jit(solution)/shard_map/while/body/eval_jaxpr/dot_general | solution.py:20
  331.3 26.1 %reduce-scatter.2.cloned.1.call-done = f32[64,1024]{1,0:T(8,128)} async-done(((f32[64,4096]{1,0:T(8,128)}), f32[64,1024]{1,0:T(8,128)}) %reduce-scatter.2.cloned.1.call-update) | async-done | bytes 262160 | tf_op jit(solution)/shard_map/while/body/eval_jaxpr/reduce_scatter | solution.py:41
  357.5 1.1 fusion.18
  358.6 5.6 %all_gather.27 = bf16[64,2048]{1,0:T(8,128)(2,1)S(1)} all-gather(bf16[64,1024]{1,0:T(8,128)(2,1)S(1)} %get-tuple-element.221), channel_id=1, replica_groups=mesh['rep'=4,'row'=2,'col'=4] {'row'}, dimensions={1}, use_global_device_ids=true | all-gather | bytes 393216 | tf_op jit(solution)/shard_map/while/body/eval_jaxpr/all_gather | solution.py:37
  364.3 9.8 %fusion.17 = f32[64,4096]{1,0:T(8,128)} fusion(bf16[64,2048]{1,0:T(8,128)(2,1)S(1)} %all_gather.27, bf16[2048,4096]{1,0:T(8,128)(2,1)} %get-tuple-element.233), kind=kOutput, calls=%fused_computation.24.clone.1 | convolution fusion | flops 1073741824 | bytes 18087936 | tf_op jit(solution)/shard_map/while/body/eval_jaxpr/dot_general | solution.py:20
  374.1 26.1 %reduce-scatter.2.cloned.1.call-done = f32[64,1024]{1,0:T(8,128)} async-done(((f32[64,4096]{1,0:T(8,128)}), f32[64,1024]{1,0:T(8,128)}) %reduce-scatter.2.cloned.1.call-update) | async-done | bytes 262160 | tf_op jit(solution)/shard_map/while/body/eval_jaxpr/reduce_scatter | solution.py:41
  401.4 5.6 %all_gather.27 = bf16[64,2048]{1,0:T(8,128)(2,1)S(1)} all-gather(bf16[64,1024]{1,0:T(8,128)(2,1)S(1)} %get-tuple-element.221), channel_id=1, replica_groups=mesh['rep'=4,'row'=2,'col'=4] {'row'}, dimensions={1}, use_global_device_ids=true | all-gather | bytes 393216 | tf_op jit(solution)/shard_map/while/body/eval_jaxpr/all_gather | solution.py:37
  407.0 9.8 %fusion.17 = f32[64,4096]{1,0:T(8,128)} fusion(bf16[64,2048]{1,0:T(8,128)(2,1)S(1)} %all_gather.27, bf16[2048,4096]{1,0:T(8,128)(2,1)} %get-tuple-element.233), kind=kOutput, calls=%fused_computation.24.clone.1 | convolution fusion | flops 1073741824 | bytes 18087936 | tf_op jit(solution)/shard_map/while/body/eval_jaxpr/dot_general | solution.py:20
  416.8 26.1 %reduce-scatter.2.cloned.1.call-done = f32[64,1024]{1,0:T(8,128)} async-done(((f32[64,4096]{1,0:T(8,128)}), f32[64,1024]{1,0:T(8,128)}) %reduce-scatter.2.cloned.1.call-update) | async-done | bytes 262160 | tf_op jit(solution)/shard_map/while/body/eval_jaxpr/reduce_scatter | solution.py:41
  443.0 1.1 fusion.18
  444.2 5.6 %all_gather.23 = bf16[64,2048]{1,0:T(8,128)(2,1)S(1)} all-gather(bf16[64,1024]{1,0:T(8,128)(2,1)S(1)} %get-tuple-element.157), channel_id=1, replica_groups=mesh['rep'=4,'row'=2,'col'=4] {'row'}, dimensions={1}, use_global_device_ids=true | all-gather | bytes 393216 | tf_op jit(solution)/shard_map/all_gather | solution.py:37
  449.8 9.8 %fusion.6 = f32[64,4096]{1,0:T(8,128)} fusion(bf16[64,2048]{1,0:T(8,128)(2,1)S(1)} %all_gather.23, bf16[2048,4096]{1,0:T(8,128)(2,1)} %get-tuple-element.241), kind=kOutput, calls=%fused_computation.25 | convolution fusion | flops 1073741824 | bytes 18087936 | tf_op jit(solution)/shard_map/dot_general | solution.py:20
  459.7 20.4 %all_gather.22 = bf16[64,4096]{1,0:T(8,128)(2,1)} all-gather(bf16[64,1024]{1,0:T(8,128)(2,1)S(1)} %get-tuple-element.157), channel_id=1, replica_groups=mesh['rep'=4,'row'=2,'col'=4] {'col'}, dimensions={1}, use_global_device_ids=true | all-gather | bytes 655360 | tf_op jit(solution)/shard_map/all_gather | solution.py:49
  483.0 32.0 %all-reduce.3.cloned.1.call-done = f32[64,4096]{1,0:T(8,128)} async-done(((f32[64,4096]{1,0:T(8,128)}), f32[64,4096]{1,0:T(8,128)}) %all-reduce.3.cloned.1.call-update) | async-done | bytes 1048592 | tf_op jit(solution)/shard_map/psum | solution.py:53
  515.0 1.6 multiply_reduce_fusion
  516.6 4.9 psum.15
  521.6 5.6 %all-reduce = f32[256]{0:T(256)S(1)} all-reduce(f32[256]{0:T(256)S(1)} %fusion.4), channel_id=1, replica_groups=mesh['rep'=4,'row'=2,'col'=4] {'rep'}, use_global_device_ids=true, to_apply=%add | all-reduce | flops 256 | bytes 2048
  528.6 3.2 gather_fusion.3
  531.8 2.0 broadcast_select_fusion
  (62 shorter events, 10.3 us)
Async XLA Ops:
  8.0 1.0 copy-start
  12.4 45.9 %reduce-scatter.2.cloned.1.call-start = ((), (), s32[]{:S(2)}) async-start(), calls=%async_computation.3 | async-start | bytes 1310720 | tf_op jit(solution)/shard_map/while/body/eval_jaxpr/reduce_scatter | solution.py:41
  59.4 41.6 %reduce-scatter.2.cloned.1.call-start = ((), (), s32[]{:S(2)}) async-start(), calls=%async_computation.3 | async-start | bytes 1310720 | tf_op jit(solution)/shard_map/while/body/eval_jaxpr/reduce_scatter | solution.py:41
  102.1 41.6 %reduce-scatter.2.cloned.1.call-start = ((), (), s32[]{:S(2)}) async-start(), calls=%async_computation.3 | async-start | bytes 1310720 | tf_op jit(solution)/shard_map/while/body/eval_jaxpr/reduce_scatter | solution.py:41
  144.9 41.7 %reduce-scatter.2.cloned.1.call-start = ((), (), s32[]{:S(2)}) async-start(), calls=%async_computation.3 | async-start | bytes 1310720 | tf_op jit(solution)/shard_map/while/body/eval_jaxpr/reduce_scatter | solution.py:41
  187.6 41.6 %reduce-scatter.2.cloned.1.call-start = ((), (), s32[]{:S(2)}) async-start(), calls=%async_computation.3 | async-start | bytes 1310720 | tf_op jit(solution)/shard_map/while/body/eval_jaxpr/reduce_scatter | solution.py:41
  230.3 41.6 %reduce-scatter.2.cloned.1.call-start = ((), (), s32[]{:S(2)}) async-start(), calls=%async_computation.3 | async-start | bytes 1310720 | tf_op jit(solution)/shard_map/while/body/eval_jaxpr/reduce_scatter | solution.py:41
  273.1 41.6 %reduce-scatter.2.cloned.1.call-start = ((), (), s32[]{:S(2)}) async-start(), calls=%async_computation.3 | async-start | bytes 1310720 | tf_op jit(solution)/shard_map/while/body/eval_jaxpr/reduce_scatter | solution.py:41
  315.8 41.6 %reduce-scatter.2.cloned.1.call-start = ((), (), s32[]{:S(2)}) async-start(), calls=%async_computation.3 | async-start | bytes 1310720 | tf_op jit(solution)/shard_map/while/body/eval_jaxpr/reduce_scatter | solution.py:41
  358.6 41.6 %reduce-scatter.2.cloned.1.call-start = ((), (), s32[]{:S(2)}) async-start(), calls=%async_computation.3 | async-start | bytes 1310720 | tf_op jit(solution)/shard_map/while/body/eval_jaxpr/reduce_scatter | solution.py:41
  401.3 41.6 %reduce-scatter.2.cloned.1.call-start = ((), (), s32[]{:S(2)}) async-start(), calls=%async_computation.3 | async-start | bytes 1310720 | tf_op jit(solution)/shard_map/while/body/eval_jaxpr/reduce_scatter | solution.py:41
  444.1 36.0 %copy-start.2 = (s32[256]{0:T(256)S(1)}, s32[256]{0:T(256)}, u32[]{:S(2)}) copy-start(s32[256]{0:T(256)} %param.13) | copy-start | bytes 3076
  444.1 36.0 %copy-start.4 = (u32[32]{0:T(128)S(1)}, u32[32]{0:T(128)}, u32[]{:S(2)}) copy-start(u32[32]{0:T(128)} %constant.92) | copy-start | bytes 388
  444.1 37.2 %copy-start.3 = (s32[256]{0:T(256)S(1)}, s32[256]{0:T(256)}, u32[]{:S(2)}) copy-start(s32[256]{0:T(256)} %param.14) | copy-start | bytes 3076
  444.1 37.3 %copy-start.1 = (f32[256]{0:T(256)S(1)}, f32[256]{0:T(256)}, u32[]{:S(2)}) copy-start(f32[256]{0:T(256)} %param.15) | copy-start | bytes 3076
  444.1 70.9 %all-reduce.3.cloned.1.call-start = ((), (), s32[]{:S(2)}) async-start(), calls=%async_computation.1 | async-start | bytes 2097152 | tf_op jit(solution)/shard_map/psum | solution.py:53
  459.6 69.0 %all-gather.2.cloned.1.call-start = ((), (), s32[]{:S(2)}) async-start(), calls=%async_computation.2 | async-start | bytes 2621440 | tf_op jit(solution)/shard_map/all_gather | solution.py:50
Sparse Core Ops, SparseCore 0:
  29.5 28.7 reduce-scatter.1
  75.0 25.9 reduce-scatter.1
  117.7 25.9 reduce-scatter.1
  160.5 26.0 reduce-scatter.1
  203.2 25.9 reduce-scatter.1
  246.0 25.9 reduce-scatter.1
  288.7 25.9 reduce-scatter.1
  331.4 25.9 reduce-scatter.1
  374.2 25.9 reduce-scatter.1
  416.9 25.9 reduce-scatter.1
  480.2 21.6 all-gather.1
Sparse Core Ops, SparseCore 1:
  459.7 55.3 all-reduce.2
where the time goes:
time: 542 us; the launch traced here: 541 us
  waiting for transfers between devices  296 us (55%)
  matrix products  107 us (20%)
  blocking collectives  94.4 us (17%)
  other arithmetic  16 us (3%)
  between operations  15.9 us (3%)
  local copies, waits for them, and re-layouts  9.87 us (2%)
    reduce_scatter x10, waiting for transfers between devices, one_sweep(): fields = lax.psum_scatter(terms, 'col', scatter_dimension=1, tiled=True)  264 us
    dot_general x11, matrix products, partial_fields(): return jnp.dot(strided, coupling_block, preferred_element_type=jnp.float32)  107 us
    all_gather x11, blocking collectives, strided_of(): return lax.all_gather(spin_state, 'row', axis=1, tiled=True)  63.5 us
    psum x1, waiting for transfers between devices, per_device(): final_local = lax.psum(final_partial, 'col')  32 us
    all_gather x1, blocking collectives, per_device(): final_rows = lax.all_gather(final_pieces, 'col', axis=1, tiled=True)  20.4 us
    convert_element_type x10, other arithmetic, metropolis(): return jnp.where(flipped, -values, values).astype(jnp.bfloat16)  10.9 us
  transfers between devices with their start and end apart: 12, of which 11 were waited for; matrix products, arithmetic and copies ran while one was open for 1% of the time, Pallas kernels for 0%

commit v1 on v0

v1 whole, which is shorter than its diff:
```python
import functools
import math

import jax
import jax.numpy as jnp
from jax import lax
from jax.experimental import pallas as pl
from jax.experimental.pallas import tpu as pltpu
from jax.sharding import PartitionSpec as P

GROUPS = 2
F8 = jnp.float8_e4m3fn
ARRIVAL = (1, 3, 2)


def metropolis(values, fields, parity, color_part, noise_part, beta_col):
    energy_cost = beta_col * (values * fields) * (1.0 / 16384.0)
    flipped = (color_part == parity) & (energy_cost < noise_part)
    return jnp.where(flipped, -values, values).astype(jnp.bfloat16)


def column_to_row(column, mask):
    return jnp.sum(jnp.where(mask, column, 0.0), axis=0, keepdims=True)


def picked(mask, row):
    return jnp.sum(jnp.where(mask, row, 0.0), axis=1, keepdims=True)


def kernel(
    sweeps, spin_count, couple_ref, init_ref, noise_ref, color_ref, beta_col_ref, beta_row_ref,
    partner_ref, swap_ref, out_ref, energy_ref,
    state, part, got, own, noise_buf, every, esend, erecv, esum,
    noise_sem, zs, zr, ys, yr, xs, xr, cs, cr, fs, fr, es, er,
):
    rep, row, col = lax.axis_index("rep"), lax.axis_index("row"), lax.axis_index("col")
    rep_dev = init_ref.shape[0]
    piece = couple_ref.shape[2]
    rows = rep_dev // GROUPS
    slots = beta_row_ref.shape[1]
    y_mate = 1 - row
    core_mate = rep + 1 - 2 * (rep % 2)
    x_mate = rep + 2 - 4 * (rep // 2)

    def at(**changes):
        return (changes.get("rep", rep), changes.get("row", row), changes.get("col", col))

    def z_of(step):
        return (col + step) % 4

    def remote(src, dst, send, recv, device):
        return pltpu.make_async_remote_copy(
            src_ref=src, dst_ref=dst, send_sem=send, recv_sem=recv,
            device_id=device, device_id_type=pl.DeviceIdType.MESH,
        )

    noise_copy = pltpu.make_async_copy(
        noise_ref.at[:, :, pl.ds(pl.multiple_of(col * piece, 128), piece)], noise_buf, noise_sem
    )
    noise_copy.start()

    partners = [at(row=y_mate), at(rep=core_mate), at(rep=x_mate)] + [at(col=z_of(d)) for d in ARRIVAL]
    barrier = pltpu.get_barrier_semaphore()
    for device in partners:
        pl.semaphore_signal(barrier, inc=1, device_id=device, device_id_type=pl.DeviceIdType.MESH)
    pl.semaphore_wait(barrier, len(partners))

    for g in range(GROUPS):
        for z in range(4):
            state[0, g, z] = init_ref[g * rows:(g + 1) * rows, z * piece:(z + 1) * piece]

    def z_copy(slot, g, step):
        return remote(
            state.at[slot, g, col], state.at[slot, g, col],
            zs.at[slot, g, step - 1], zr.at[slot, g, step - 1], at(col=z_of(step)),
        )

    def y_copy(slot, g):
        return remote(part.at[slot, g], got.at[slot, g], ys.at[slot, g], yr.at[slot, g], at(row=y_mate))

    def product(slot, g, z, half):
        return jnp.dot(
            state[slot, g, z].astype(F8), couple_ref[z, half], preferred_element_type=jnp.float32
        )

    def x_copy(g, z, lane):
        return remote(
            state.at[0, g, z], every.at[z, rep, g], xs.at[lane, g], xr.at[lane, g], at(rep=x_mate)
        )

    def c_copy(g, z, lane):
        return remote(
            state.at[0, g, z], every.at[z, rep, g], cs.at[lane, g], cr.at[lane, g], at(rep=core_mate)
        )

    def f_copy(g, z, lane):
        return remote(
            every.at[z, x_mate, g], every.at[z, x_mate, g], fs.at[lane, g], fr.at[lane, g],
            at(rep=core_mate),
        )

    def matmuls(slot, g, first, last):
        def share(step, lane):
            if last:
                z = z_of(step)
                x_copy(g, z, step).start()
                c_copy(g, z, step).start()

        share(0, 0)
        total = product(slot, g, col, y_mate)
        for step in ARRIVAL:
            if not first:
                z_copy(slot, g, 4 - step).wait_recv()
            share(step, step)
            total += product(slot, g, z_of(step), y_mate)
        part[slot, g] = total.astype(jnp.int32).astype(jnp.int16)
        y_copy(slot, g).start()
        total = product(slot, g, col, row)
        for step in ARRIVAL:
            total += product(slot, g, z_of(step), row)
        own[g] = total
        if not first:
            for step in ARRIVAL:
                z_copy(slot, g, step).wait_send()

    def fields_of(slot, g):
        y_copy(slot, g).wait_recv()
        fields = own[g] + got[slot, g].astype(jnp.int32).astype(jnp.float32)
        y_copy(slot, g).wait_send()
        return fields

    def update(k, slot, g):
        fields = fields_of(slot, g)
        beta = beta_col_ref[pl.ds(pl.multiple_of(rep * rep_dev + g * rows, 8), rows), :].astype(jnp.float32)
        later = 1 - slot
        state[later, g, col] = metropolis(
            state[slot, g, col].astype(jnp.float32), fields, slot, color_ref[col],
            noise_buf[k, g * rows:(g + 1) * rows, :], beta,
        )
        for step in ARRIVAL:
            z_copy(later, g, step).start()

    def sweep(k, slot, first=False):
        for g in range(GROUPS):
            matmuls(slot, g, first, False)
        if first:
            noise_copy.wait()
        for g in range(GROUPS):
            update(k, slot, g)

    sweep(0, 0, True)

    def body(k, carry):
        sweep(k, k % 2)
        return carry

    lax.fori_loop(1, sweeps, body, 0)

    for g in range(GROUPS):
        matmuls(0, g, False, True)
    sums = []
    for g in range(GROUPS):
        fields = fields_of(0, g)
        sums.append(jnp.sum(state[0, g, col].astype(jnp.float32) * fields, axis=1, keepdims=True))
    lanes = lax.broadcasted_iota(jnp.int32, (rep_dev, slots), 1)
    ids = rep * rep_dev + lax.broadcasted_iota(jnp.int32, (rep_dev, 1), 0)
    mine = lanes == ids
    total = column_to_row(jnp.concatenate(sums, axis=0), mine)

    stages = (
        (at(row=y_mate),),
        tuple(at(col=z_of(d)) for d in (1, 2, 3)),
        (at(rep=core_mate),),
        (at(rep=x_mate),),
    )
    place = 0
    for number, stage in enumerate(stages):
        esend[number] = jnp.broadcast_to(total, esend.shape[1:])
        copies = []
        for device in stage:
            copies.append(remote(esend.at[number], erecv.at[place], es.at[place], er.at[place], device))
            copies[-1].start()
            place += 1
        if number == 1:
            for g in range(GROUPS):
                for step in (0,) + ARRIVAL:
                    z = z_of(step)
                    x_copy(g, z, step).wait_recv()
                    f_copy(g, z, step).start()
        for offset, copy in enumerate(copies):
            copy.wait_recv()
            total += erecv[place - len(stage) + offset, 0:1, :]
        for copy in copies:
            copy.wait_send()

    mate_ids = partner_ref[pl.ds(pl.multiple_of(rep * rep_dev, 8), rep_dev), :]
    mate = lanes == mate_ids
    betas = beta_row_ref[...].astype(jnp.float32)
    energy_row = -0.5 * total
    mate_energy, energy = picked(mate, energy_row), picked(mine, energy_row)
    swap_gain = (
        (picked(mine, betas) - picked(mate, betas))
        * (energy - mate_energy)
        * (1.0 / (64.0 * spin_count * math.sqrt(spin_count)))
    )
    accept = swap_gain + picked(lanes == jnp.minimum(ids, mate_ids), swap_ref[...]) > 0.0
    scale = 1.0 / (spin_count * math.sqrt(spin_count))
    local = lax.broadcasted_iota(jnp.int32, (rep_dev, rep_dev), 1) == lax.broadcasted_iota(
        jnp.int32, (rep_dev, rep_dev), 0
    )
    energy_ref[...] = column_to_row(jnp.where(accept, mate_energy, energy) * scale, local)
    taken = (lanes == jnp.where(accept, mate_ids, ids)).astype(jnp.float32).astype(jnp.bfloat16)

    for g in range(GROUPS):
        for step in (0,) + ARRIVAL:
            z = z_of(step)
            every[z, rep, g] = state[0, g, z]
            c_copy(g, z, step).wait_recv()
            f_copy(g, z, step).wait_recv()
            x_copy(g, z, step).wait_send()
            c_copy(g, z, step).wait_send()
            f_copy(g, z, step).wait_send()
    for z in range(4):
        out_ref[:, z * piece:(z + 1) * piece] = jnp.dot(
            taken, every[z].reshape(slots, piece), preferred_element_type=jnp.float32
        ).astype(jnp.bfloat16)


def fused(sweeps, spin_count, spin_init, couplings, flip_noise, colors, beta_steps, partners, swap_noise):
    rep_dev, row_width = spin_init.shape
    row_count, _, piece, _ = couplings.shape
    slots = beta_steps.shape[0]
    rows = rep_dev // GROUPS
    block = couplings.astype(F8).reshape(row_count, piece, 4, piece)
    block = jnp.transpose(block, (2, 0, 3, 1))
    vmem = pl.BlockSpec(memory_space=pltpu.VMEM)
    dma = pltpu.SemaphoreType.DMA
    spins_out, energies = pl.pallas_call(
        functools.partial(kernel, sweeps, spin_count),
        out_shape=(
            jax.ShapeDtypeStruct((rep_dev, row_width), jnp.bfloat16),
            jax.ShapeDtypeStruct((1, rep_dev), jnp.float32),
        ),
        in_specs=[vmem, vmem, pl.BlockSpec(memory_space=pl.ANY)] + [vmem] * 5,
        out_specs=(vmem, vmem),
        scratch_shapes=[
            pltpu.VMEM((2, GROUPS, 4, rows, piece), jnp.bfloat16),
            pltpu.VMEM((2, GROUPS, rows, piece), jnp.int16),
            pltpu.VMEM((2, GROUPS, rows, piece), jnp.int16),
            pltpu.VMEM((GROUPS, rows, piece), jnp.float32),
            pltpu.VMEM((sweeps, rep_dev, piece), jnp.float32),
            pltpu.VMEM((4, 4, GROUPS, rows, piece), jnp.bfloat16),
            pltpu.VMEM((4, 8, slots), jnp.float32),
            pltpu.VMEM((6, 8, slots), jnp.float32),
            pltpu.VMEM((8, slots), jnp.float32),
            dma,
            dma((2, GROUPS, 3)), dma((2, GROUPS, 3)),
            dma((2, GROUPS)), dma((2, GROUPS)),
            dma((4, GROUPS)), dma((4, GROUPS)),
            dma((4, GROUPS)), dma((4, GROUPS)),
            dma((4, GROUPS)), dma((4, GROUPS)),
            dma((6,)), dma((6,)),
        ],
        compiler_params=pltpu.CompilerParams(
            collective_id=0, has_side_effects=True, vmem_limit_bytes=56 * 2**20
        ),
    )(
        block, spin_init, flip_noise, colors.reshape(4, 1, piece), beta_steps.reshape(slots, 1),
        beta_steps.reshape(1, slots), partners.reshape(slots, 1), swap_noise.reshape(1, slots),
    )
    return spins_out, energies.reshape(rep_dev)


def general(sweeps, spin_count, spin_init, couplings, flip_noise, colors, beta_steps, partners, swap_noise):
    rep_dev, row_width = spin_init.shape
    col_index = lax.axis_index("col")
    rep_index = lax.axis_index("rep")
    piece_size = row_width // lax.axis_size("col")
    coupling_block = couplings.reshape(-1, row_width)
    own_slots = functools.partial(lax.dynamic_slice_in_dim, start_index=rep_index * rep_dev, slice_size=rep_dev)
    beta_col = own_slots(beta_steps).astype(jnp.float32)[:, None]
    color_part = lax.dynamic_slice_in_dim(colors, col_index * piece_size, piece_size)
    noise_part = lax.dynamic_slice_in_dim(flip_noise, col_index * piece_size, piece_size, 2)

    def partial_fields(spin_state):
        strided = lax.all_gather(spin_state, "row", axis=1, tiled=True)
        return jnp.dot(strided, coupling_block, preferred_element_type=jnp.float32)

    def summed(spin_state):
        return lax.psum_scatter(partial_fields(spin_state), "col", scatter_dimension=1, tiled=True)

    def one_sweep(k, spin_state):
        return metropolis(
            spin_state.astype(jnp.float32), summed(spin_state), k % 2, color_part[None, :], noise_part[k], beta_col
        )

    start = lax.dynamic_slice_in_dim(spin_init, col_index * piece_size, piece_size, 1)
    final = lax.fori_loop(0, sweeps, one_sweep, start)
    final_rows = lax.all_gather(final, "col", axis=1, tiled=True)
    every_spins = lax.all_gather(final_rows, "rep", axis=0, tiled=True)
    energy = -0.5 * lax.psum(jnp.sum(final.astype(jnp.float32) * summed(final), axis=1), ("row", "col"))
    every_energy = lax.all_gather(energy, "rep", axis=0, tiled=True)
    slot_ids = rep_index * rep_dev + jnp.arange(rep_dev, dtype=jnp.int32)
    mate_ids = own_slots(partners)
    all_betas = beta_steps.astype(jnp.float32)
    mate_energy = every_energy[mate_ids]
    swap_gain = (
        (beta_col[:, 0] - all_betas[mate_ids])
        * (energy - mate_energy)
        * (1.0 / (64.0 * spin_count * math.sqrt(spin_count)))
    )
    accept = swap_gain + swap_noise[jnp.minimum(slot_ids, mate_ids)] > 0.0
    spins_out = jnp.where(accept[:, None], every_spins[mate_ids], final_rows)
    energies = jnp.where(accept, mate_energy, energy) * (1.0 / (spin_count * math.sqrt(spin_count)))
    return (spins_out, energies)


def per_device(spin_init, couplings, flip_noise, *others):
    axes = tuple(lax.axis_size(name) for name in ("rep", "row", "col"))
    rep_dev, row_width = spin_init.shape
    sweeps = flip_noise.shape[0]
    fits = axes == (4, 2, 4) and row_width % 512 == 0 and rep_dev % (32 * GROUPS) == 0
    fits = fits and sweeps % 2 == 0 and couplings.shape[0] == 2 and couplings.nbytes <= 2**24
    run = fused if fits else general
    return run(sweeps, row_width * axes[1], spin_init, couplings, flip_noise, *others)


def solution(mesh):
    in_specs = (
        P("rep", "row"),
        P(None, "col", None, "row"),
        P(None, "rep", "row"),
        P("row"),
        P(),
        P(),
        P(),
    )
    out_specs = (P("rep", "row"), P("rep"))
    return jax.shard_map(
        per_device, mesh=mesh, in_specs=in_specs, out_specs=out_specs, check_vma=False
    )
```

time: 542 us -> 199 us (0.37)
  waiting for transfers between devices: 296 us -> 0 us
  Pallas kernels: 0 us -> 156 us
  matrix products: 107 us -> 0 us
  blocking collectives: 94.4 us -> 0 us
  local copies, waits for them, and re-layouts: 9.87 us -> 33.5 us
  between operations: 15.9 us -> 0.66 us
  other arithmetic: 16 us -> 8.64 us
    reduce_scatter x10 -> x0, waiting for transfers between devices: 264 us -> none  [one_sweep(): fields = lax.psum_scatter(terms, 'col', scatter_dimension=1, tiled=True)]
    pallas_call x0 -> x1, Pallas kernels: none -> 156 us  [fused(): pl.pallas_call(functools.partial(kernel, sweeps, spin_count), out_shape=(...]
    dot_general x11 -> x0, matrix products: 107 us -> none  [partial_fields(): return jnp.dot(strided, coupling_block, preferred_element_type=jnp.float32)]
    all_gather x12 -> x0, blocking collectives: 83.9 us -> none  [the longest x11 63.5 us: strided_of(): return lax.all_gather(spin_state, 'row', axis=1, tiled=True)]
    psum x1 -> x0, waiting for transfers between devices: 32 us -> none  [per_device(): final_local = lax.psum(final_partial, 'col')]
    unnamed x12 -> x7, local copies, waits for them, and re-layouts: 1.65 us -> 24.3 us
    reshape x0 -> x3, local copies, waits for them, and re-layouts: none -> 9.21 us  [the longest x1 7.62 us: fused(): block = couplings.astype(F8).reshape(row_count, piece, 4, piece)]
    unnamed x1 -> x0, blocking collectives: 5.63 us -> none
  transfers between devices with their start and end apart: 12 -> 0, of which waited for: 11 -> 0; matrix products, arithmetic and copies ran while one was open for 1% -> 0% of each run, Pallas kernels for 0% -> 0%
where the time goes in v1:
time: 199 us
  Pallas kernels  156 us (78%)
  local copies, waits for them, and re-layouts  33.5 us (17%)
  other arithmetic  8.64 us (4%)
    pallas_call x1, Pallas kernels, fused(): pl.pallas_call(functools.partial(kernel, sweeps, spin_count), out_shape=(...  156 us
    unnamed x7, local copies, waits for them, and re-layouts  24.3 us
    convert_element_type x1, other arithmetic, fused(): block = couplings.astype(F8).reshape(row_count, piece, 4, piece)  8.64 us
    reshape x1, local copies, waits for them, and re-layouts, fused(): block = couplings.astype(F8).reshape(row_count, piece, 4, piece)  7.62 us

profile of v1, /device:TPU:0, one launch (start us, length us, event | category | flops | bytes accessed | tf_op | source)
XLA Modules:
  0.0 198.8 jit_solution(16483029838454013781)
XLA Ops:
  0.6 21.2 %copy.9 = bf16[2,1,1024,4096]{2,3,0,1:T(8,128)(2,1)} copy(bf16[2,1,1024,4096]{3,2,1,0:T(8,128)(2,1)} %param.8) | data formatting | bytes 33554432 | tf_op args[1]
  21.8 8.6 %convert_element_type.3 = f8e4m3fn[2,1,1024,4096]{2,3,0,1:T(32,128)(4,1)S(1)} convert(bf16[2,1,1024,4096]{2,3,0,1:T(8,128)(2,1)} %copy.9) | non-fusion elementwise | flops 8388608 | bytes 25165824 | tf_op jit(solution)/shard_map/convert_element_type | solution.py:234
  30.5 0.0 copy-start
  30.5 0.0 copy-start.1
  30.5 7.6 %copy.14 = f8e4m3fn[2,1024,4,1024]{1,3,0,2:T(32,128)(4,1)} copy(f8e4m3fn[2,1024,4,1024]{1,3,2,0:T(32,128)(4,1)S(1)} %bitcast.10) | data formatting | bytes 16777216 | tf_op jit(solution)/shard_map/reshape | solution.py:234
  38.1 0.0 copy-done
  38.1 0.8 copy.11.beta_col_ref
  38.9 0.0 copy-done.1
  38.9 0.8 copy.12.partner_ref
  39.7 156.0 %shard_map.86 = (bf16[64,4096]{1,0:T(8,128)(2,1)}, f32[1,64]{1,0:T(1,128)}) custom-call(f8e4m3fn[4,2,1024,1024]{3,2,1,0:T(32,128)(4,1)} %bitcast.11, bf16[64,4096]{1,0:T(8,128)(2,1)} %init_ref.1, f32[10,64,4096]{2,1,0:T(8,128)} %noise_ref.1, s32[4,1,1024]{2,1,0:T(1,128)} %bitcast.12, s32[256,1]{1,0:T(8,128)} %copy.11.beta_col_ref, s32[1,256]{1,0:T(1,128)} %bitcast.13, ...), custom_call_target="tpu_custom_call" | custom-call | tf_op jit(solution)/shard_map/pallas_call | solution.py:238
  195.8 1.9 copy.17
  197.6 1.2 copy.18
Async XLA Ops:
  30.5 7.6 %copy-start = (s32[256]{0:T(256)S(1)}, s32[256]{0:T(256)}, u32[]{:S(2)}) copy-start(s32[256]{0:T(256)} %param.11) | copy-start | bytes 3076
  30.5 8.4 %copy-start.1 = (s32[256]{0:T(256)S(1)}, s32[256]{0:T(256)}, u32[]{:S(2)}) copy-start(s32[256]{0:T(256)} %param.12) | copy-start | bytes 3076

commit v2 on v1

--- a/solution.py
+++ b/solution.py
@@ -28,14 +28,14 @@
 
 
 def kernel(
-    sweeps, spin_count, couple_ref, init_ref, noise_ref, color_ref, beta_col_ref, beta_row_ref,
+    sweeps, spin_count, matrix_ref, init_ref, noise_ref, color_ref, beta_col_ref, beta_row_ref,
     partner_ref, swap_ref, out_ref, energy_ref,
     state, part, got, own, noise_buf, every, esend, erecv, esum,
-    noise_sem, zs, zr, ys, yr, xs, xr, cs, cr, fs, fr, es, er,
+    couple_ref, matrix_buf, matrix_sem, noise_sem, zs, zr, ys, yr, xs, xr, cs, cr, fs, fr, es, er,
 ):
     rep, row, col = lax.axis_index("rep"), lax.axis_index("row"), lax.axis_index("col")
     rep_dev = init_ref.shape[0]
-    piece = couple_ref.shape[2]
+    piece = matrix_ref.shape[2]
     rows = rep_dev // GROUPS
     slots = beta_row_ref.shape[1]
     y_mate = 1 - row
@@ -59,6 +59,14 @@
     )
     noise_copy.start()
 
+    def matrix_copy(z):
+        return pltpu.make_async_copy(
+            matrix_ref.at[:, 0, :, pl.ds(z * piece, piece)], matrix_buf.at[z % 2], matrix_sem.at[z % 2]
+        )
+
+    matrix_copy(0).start()
+    matrix_copy(1).start()
+
     partners = [at(row=y_mate), at(rep=core_mate), at(rep=x_mate)] + [at(col=z_of(d)) for d in ARRIVAL]
     barrier = pltpu.get_barrier_semaphore()
     for device in partners:
@@ -68,6 +76,25 @@
     for g in range(GROUPS):
         for z in range(4):
             state[0, g, z] = init_ref[g * rows:(g + 1) * rows, z * piece:(z + 1) * piece]
+
+    tile = 256
+    unit = lax.broadcasted_iota(jnp.int32, (tile, tile), 0) == lax.broadcasted_iota(jnp.int32, (tile, tile), 1)
+    unit = unit.astype(jnp.float32).astype(jnp.bfloat16)
+    for z in range(4):
+        matrix_copy(z).wait()
+
+        def turn(index, carry):
+            span = pl.ds(pl.multiple_of(index * tile, tile), tile)
+            for half in range(2):
+                couple_ref[z, half, span, :] = lax.dot_general(
+                    unit, matrix_buf[z % 2, half, :, span], (((1,), (1,)), ((), ())),
+                    preferred_element_type=jnp.float32,
+                ).astype(F8)
+            return carry
+
+        lax.fori_loop(0, piece // tile, turn, 0)
+        if z < 2:
+            matrix_copy(z + 2).start()
 
     def z_copy(slot, g, step):
         return remote(
@@ -231,9 +258,8 @@
     row_count, _, piece, _ = couplings.shape
     slots = beta_steps.shape[0]
     rows = rep_dev // GROUPS
-    block = couplings.astype(F8).reshape(row_count, piece, 4, piece)
-    block = jnp.transpose(block, (2, 0, 3, 1))
     vmem = pl.BlockSpec(memory_space=pltpu.VMEM)
+    hbm = pl.BlockSpec(memory_space=pl.ANY)
     dma = pltpu.SemaphoreType.DMA
     spins_out, energies = pl.pallas_call(
         functools.partial(kernel, sweeps, spin_count),
@@ -241,7 +267,7 @@
             jax.ShapeDtypeStruct((rep_dev, row_width), jnp.bfloat16),
             jax.ShapeDtypeStruct((1, rep_dev), jnp.float32),
         ),
-        in_specs=[vmem, vmem, pl.BlockSpec(memory_space=pl.ANY)] + [vmem] * 5,
+        in_specs=[hbm, vmem, hbm] + [vmem] * 5,
         out_specs=(vmem, vmem),
         scratch_shapes=[
             pltpu.VMEM((2, GROUPS, 4, rows, piece), jnp.bfloat16),
@@ -253,6 +279,9 @@
             pltpu.VMEM((4, 8, slots), jnp.float32),
             pltpu.VMEM((6, 8, slots), jnp.float32),
             pltpu.VMEM((8, slots), jnp.float32),
+            pltpu.VMEM((4, row_count, piece, piece), F8),
+            pltpu.VMEM((2, row_count, piece, piece), jnp.bfloat16),
+            dma((2,)),
             dma,
             dma((2, GROUPS, 3)), dma((2, GROUPS, 3)),
             dma((2, GROUPS)), dma((2, GROUPS)),
@@ -265,7 +294,7 @@
             collective_id=0, has_side_effects=True, vmem_limit_bytes=56 * 2**20
         ),
     )(
-        block, spin_init, flip_noise, colors.reshape(4, 1, piece), beta_steps.reshape(slots, 1),
+        couplings, spin_init, flip_noise, colors.reshape(4, 1, piece), beta_steps.reshape(slots, 1),
         beta_steps.reshape(1, slots), partners.reshape(slots, 1), swap_noise.reshape(1, slots),
     )
     return spins_out, energies.reshape(rep_dev)
@@ -319,7 +348,7 @@
     axes = tuple(lax.axis_size(name) for name in ("rep", "row", "col"))
     rep_dev, row_width = spin_init.shape
     sweeps = flip_noise.shape[0]
-    fits = axes == (4, 2, 4) and row_width % 512 == 0 and rep_dev % (32 * GROUPS) == 0
+    fits = axes == (4, 2, 4) and row_width % 1024 == 0 and rep_dev % (32 * GROUPS) == 0
     fits = fits and sweeps % 2 == 0 and couplings.shape[0] == 2 and couplings.nbytes <= 2**24
     run = fused if fits else general
     return run(sweeps, row_width * axes[1], spin_init, couplings, flip_noise, *others)

time: 199 us -> 167 us (0.84)
  local copies, waits for them, and re-layouts: 33.5 us -> 5.98 us
  other arithmetic: 8.64 us -> 0 us
  Pallas kernels: 156 us -> 160 us
    unnamed x7 -> x2, local copies, waits for them, and re-layouts: 24.3 us -> 3.04 us
    convert_element_type x1 -> x0, other arithmetic: 8.64 us -> none  [fused(): block = couplings.astype(F8).reshape(row_count, piece, 4, piece)]
    reshape x1 -> x0, local copies, waits for them, and re-layouts: 7.62 us -> none  [fused(): block = couplings.astype(F8).reshape(row_count, piece, 4, piece)]
    pallas_call x1, Pallas kernels: 156 us -> 160 us  [fused(): pl.pallas_call(functools.partial(kernel, sweeps, spin_count), out_shape=(...]
where the time goes in v2:
time: 167 us
  Pallas kernels  160 us (96%)
  local copies, waits for them, and re-layouts  5.98 us (4%)
    pallas_call x1, Pallas kernels, fused(): pl.pallas_call(functools.partial(kernel, sweeps, spin_count), out_shape=(...  160 us

profile of v2, /device:TPU:0, one launch (start us, length us, event | category | flops | bytes accessed | tf_op | source)
XLA Modules:
  0.0 167.1 jit_solution(17576160666371131116)
XLA Ops:
  0.6 1.5 copy.10.partner_ref
  2.1 1.5 copy.9.beta_col_ref
  3.6 160.4 %shard_map.86 = (bf16[64,4096]{1,0:T(8,128)(2,1)}, f32[1,64]{1,0:T(1,128)}) custom-call(bf16[2,1,1024,4096]{3,2,1,0:T(8,128)(2,1)} %matrix_ref.1, bf16[64,4096]{1,0:T(8,128)(2,1)} %init_ref.1, f32[10,64,4096]{2,1,0:T(8,128)} %noise_ref.1, s32[4,1,1024]{2,1,0:T(1,128)} %bitcast.6, s32[256,1]{1,0:T(8,128)} %copy.9.beta_col_ref, s32[1,256]{1,0:T(1,128)} %bitcast.8, ...), custom_call_target="tpu_custom_call" | custom-call | tf_op jit(solution)/shard_map/pallas_call | solution.py:264
  164.0 1.9 %copy.13 = bf16[64,4096]{1,0:T(8,128)(2,1)} copy(bf16[64,4096]{1,0:T(8,128)(2,1)} %get-tuple-element.8) | data formatting | bytes 1048576
  165.9 1.2 copy.14
